TPU v7x, 1024 devices: a whole 8x8x8 slice. The times are simulated.
1024 devices in a mesh: grid: 64 (over x, z_lo, core), shard: 16 (over y, z_hi).
Axes of the slice: x: 8, y: 8, z: 8 (z_hi: 2, z_lo: 4; z = z_hi * 4 + z_lo), core: 2. Of those that a mesh axis runs over, the one named last changes fastest.
Arguments:
- density: float32 [64, 256, 16, 512], P('grid', 'shard'), may hold values from -1.6 to 1.6
- coefficients: int32 [64], P('grid'), may hold values from -2 to 2
- offsets: int32 [64, 6], P('grid'), may hold values from 0 to 3
- fractions: float32 [64, 6], P('grid'), may hold values from 0.05 to 0.95
- subspace_ids: int32 [64, 256, 16], P('grid', 'shard'), may hold values from 0 to 1023, as said below
Outputs:
- combined: float32 [64, 256, 16, 512], P('grid', 'shard')
Inputs may be any that keep to these rules, and one draw needn't show every extreme that they name: `subspace_ids`: cut each grid's blocks b = i0 * 16 + i1 into runs of 256 consecutive blocks. Within one run at most 8 ids lie in any one range r * 16 to r * 16 + 15, and in every run one such range, the same for all grids at that run, holds exactly 8.
All inputs are finite; a program needn't handle non-finite values.
Results may differ from a plain program's by a relative error of at most 0.0003.
Values sent between devices are 32-bit elements; how exact they have to be, the bound alone decides.
A program may use at most 128 MiB of HBM per device.

v0:
```python
from functools import reduce

import jax
import jax.numpy as jnp
import numpy as np
from jax import lax
from jax.sharding import Mesh
from jax.sharding import PartitionSpec as P

M2 = 8
M3 = 4
M4 = 4
M5 = 4
OWN = 16
GRID = ("grid_0", "grid_1", "grid_2")


highest = lax.Precision.HIGHEST


def side_by_side(arrays, axis, split_dim, concat_dim, along):
    columns = [a.reshape(*a.shape[:along], -1) for a in arrays]
    both = jnp.concatenate(columns, axis=along)
    result, at, finished = (
        lax.all_to_all(both, axis, split_axis=split_dim, concat_axis=concat_dim, tiled=True),
        0,
        [],
    )
    for a, column in zip(arrays, columns):
        piece = result[..., at : at + column.shape[along]]
        finished.append(piece.reshape(*piece.shape[:along], *a.shape[along:]))
        at += column.shape[along]
    return tuple(finished)


def cut_along(shard, dim, peers):
    before, after = (shard.shape[:dim], shard.shape[dim + 1 :])
    return jnp.moveaxis(shard.reshape(*before, peers, -1, *after), dim, 0)


def joined_along(pieces, dim):
    shape = list(pieces.shape[1:])
    shape[dim] *= pieces.shape[0]
    return jnp.moveaxis(pieces, 0, dim).reshape(shape)


def exchange_in_order(pieces, axes, order):
    shape = [lax.axis_size(a) for a in axes]
    pieces = pieces.reshape(*shape, *pieces.shape[1:])
    for k in order:
        pieces = lax.all_to_all(pieces, axes[k], split_axis=k, concat_axis=k, tiled=True)
    return pieces.reshape(-1, *pieces.shape[len(axes) :])


def exchange_by_chip(shard, groups, order, split_dim, concat_dim):
    peers = lax.axis_size(groups[0]) * lax.axis_size(groups[1])
    pieces = cut_along(shard, split_dim, peers)
    return joined_along(exchange_in_order(pieces, groups, order), concat_dim)


def hier_table(length):
    matrix = np.eye(length)
    for level_index in range(length.bit_length() - 1):
        spacing = 2**level_index
        for position in range(spacing, length, 2 * spacing):
            matrix[position] = matrix[position] - 0.5 * (
                matrix[position - spacing] + matrix[(position + spacing) % length]
            )
    return matrix.astype(np.float32)


def dehier_table(length):
    matrix = np.eye(length)
    for level_index in reversed(range(length.bit_length() - 1)):
        spacing = 2**level_index
        for position in range(spacing, length, 2 * spacing):
            matrix[position] = matrix[position] + 0.5 * (
                matrix[position - spacing] + matrix[(position + spacing) % length]
            )
    return matrix.astype(np.float32)


def sweep_matrix(length, shift, fraction):
    row_index = jnp.arange(length, dtype=jnp.int32)[:, None]
    column_index = jnp.arange(length, dtype=jnp.int32)[None, :]
    remain = 1.0 - fraction
    weights = (
        -remain * (remain - 1.0) * (remain - 2.0) / 6.0,
        (remain + 1.0) * (remain - 1.0) * (remain - 2.0) / 2.0,
        -(remain + 1.0) * remain * (remain - 2.0) / 2.0,
        (remain + 1.0) * remain * (remain - 1.0) / 6.0,
    )
    matrix = jnp.zeros((length, length), jnp.float32)
    for stencil, weight in enumerate(weights):
        source = jnp.mod(row_index - shift - 2 + stencil, length)
        matrix = matrix + jnp.where(source == column_index, weight, 0.0)
    return matrix


def operator_pair(length, shift, fraction):
    return jnp.dot(
        jnp.asarray(hier_table(length)), sweep_matrix(length, shift, fraction), precision=highest
    )


def kron_pair(left_matrix, right_matrix):
    return jnp.kron(left_matrix, right_matrix)


def apply_tail(volume, tail_matrix):
    return jnp.einsum("abx,tx->abt", volume, tail_matrix, precision=highest)


def transform(volume, lead_matrix, second_matrix, tail_matrix):
    volume = jnp.einsum("axt,bx->abt", volume, second_matrix, precision=highest)
    pencil = lax.all_to_all(volume, "shard", split_axis=1, concat_axis=0, tiled=True)
    pencil = jnp.einsum("xbt,ax->abt", pencil, lead_matrix, precision=highest)
    pencil = apply_tail(pencil, tail_matrix)
    return lax.all_to_all(pencil, "shard", split_axis=0, concat_axis=1, tiled=True)


def body(density, coefficients, offsets, fractions, subspace_ids):
    volume = density[0]
    lead_rows, second_len, tail_len = volume.shape
    shards = lax.axis_size("shard")
    groups = lax.axis_size(GRID)
    lead_len = lead_rows * shards
    blocks = lead_rows * second_len
    shifts = offsets[0]
    fraction_row = fractions[0]
    tail_shape = (M2, M3, M4, M5)
    lead_forward = operator_pair(lead_len, shifts[0], fraction_row[0])
    second_forward = operator_pair(second_len, shifts[1], fraction_row[1])
    tail_forward = reduce(
        kron_pair,
        [
            operator_pair(tail_shape[which], shifts[which + 2], fraction_row[which + 2])
            for which in range(4)
        ],
    )
    lead_backward = jnp.asarray(dehier_table(lead_len))
    second_backward = jnp.asarray(dehier_table(second_len))
    tail_backward = jnp.asarray(reduce(np.kron, [dehier_table(length) for length in tail_shape]))
    hierarchized = transform(volume, lead_forward, second_forward, tail_forward)
    signed_rows = hierarchized.reshape(blocks, tail_len) * coefficients[0].astype(jnp.float32)
    block_ids = subspace_ids[0].reshape(blocks)
    capacity = max(2, 2 * blocks // groups)
    slot_count = capacity * groups
    owner = block_ids // OWN
    owner_hot = (owner[:, None] == jnp.arange(groups, dtype=jnp.int32)[None, :]).astype(jnp.int32)
    earlier = jnp.cumsum(owner_hot, axis=0) - owner_hot
    rank = jnp.sum(earlier * owner_hot, axis=1)
    slot = owner * capacity + rank
    placing = (jnp.arange(slot_count, dtype=jnp.int32)[:, None] == slot[None, :]).astype(
        jnp.float32
    )
    outgoing = jnp.dot(placing, signed_rows, precision=highest, preferred_element_type=jnp.float32)
    labels = jnp.dot(placing, (block_ids % OWN + 1).astype(jnp.float32), precision=highest)
    arrived, arrived_labels = side_by_side((outgoing, labels), GRID, 0, 0, 1)
    keeper = (
        (jnp.arange(OWN, dtype=jnp.int32) + 1).astype(jnp.float32)[:, None]
        == arrived_labels[None, :]
    ).astype(jnp.float32)
    owned = jnp.dot(keeper, arrived, precision=highest, preferred_element_type=jnp.float32)
    answers = jnp.dot(keeper.T, owned, precision=highest, preferred_element_type=jnp.float32)
    returned = exchange_by_chip(answers, (("grid_0", "grid_1"), "grid_2"), (1, 0), 0, 0)
    combined_rows = jnp.dot(
        placing.T, returned, precision=highest, preferred_element_type=jnp.float32
    )
    combined = transform(
        combined_rows.reshape(lead_rows, second_len, tail_len),
        lead_backward,
        second_backward,
        tail_backward,
    )
    return combined[None]


def solution(mesh):
    torus = Mesh(
        mesh.devices.reshape(8, 4, 2, mesh.shape["shard"]), ("grid_0", "grid_1", "grid_2", "shard")
    )
    in_specs = (
        P(GRID, "shard", None, None),
        P(GRID),
        P(GRID, None),
        P(GRID, None),
        P(GRID, "shard", None),
    )
    out_specs = P(GRID, "shard", None, None)
    return jax.shard_map(body, mesh=torus, in_specs=in_specs, out_specs=out_specs, check_vma=False)
```

profile of v0, /device:TPU:1, one launch (start us, length us, event | category | flops | bytes accessed | tf_op | source)
XLA Modules:
  0.0 275.4 jit_solution(12804266153499365795)
XLA Ops:
  0.0 1.6 fusion.156
  2.9 1.5 fusion.155
  4.4 0.6 and_select_fusion.16
  5.0 0.6 and_select_fusion.18
  6.9 0.9 convolution_bitcast_fusion.5
  7.8 0.6 convolution_bitcast_fusion.3
  8.4 1.1 copy.50
  9.5 20.3 %all-to-all-start = ((f32[16,16,512]{2,0,1:T(8,128)}), f32[16,16,512]{2,0,1:T(8,128)S(1)}, u32[]{:S(2)}, u32[]{:S(2)}) async-start(f32[16,16,512]{2,0,1:T(8,128)} %copy.50), calls=%async_computation | async-start | bytes 1048576 | tf_op jit(solution)/shard_map/all_to_all | solution.py:116
  32.5 0.7 and_select_fusion.12
  33.2 0.7 and_select_fusion.14
  36.4 0.6 and_select_fusion.8
  37.0 0.6 and_select_fusion.10
  40.5 0.6 and_select_fusion.4
  41.1 0.6 and_select_fusion.6
  44.5 0.6 and_select_fusion
  45.1 0.6 and_select_fusion.2
  46.5 0.3 broadcast_multiply_fusion.1
  46.8 1.6 mul.302
  48.8 11.3 %broadcast_multiply_fusion = f32[128,4,128,4]{3,2,1,0:T(8,128)} fusion(f32[4,4]{1,0:T(4,128)S(1)} %fusion.65, f32[128,128]{1,0:T(8,128)S(1)} %mul.302), kind=kLoop, calls=%fused_computation | loop fusion | flops 262144 | bytes 1114176 | tf_op jit(solution)/shard_map/jit(kron)/mul | solution.py:107
  63.0 28.8 %mul.314 = f32[512,512]{1,0:T(8,128)S(1)} reshape(f32[128,4,128,4]{3,2,1,0:T(8,128)} %broadcast_multiply_fusion) | data formatting | bytes 2097152 | tf_op jit(solution)/shard_map/jit(kron)/mul | solution.py:107
  92.4 0.6 reduce-window.6
  93.0 0.7 and_select_fusion.20
  93.7 0.6 and_select_fusion.22
  94.4 0.8 fusion.6
  95.1 0.6 fusion.157
  95.8 1.1 convolution_bitcast_fusion.2
  96.8 1.3 copy.51
  98.2 11.5 %all-to-all-start.1 = ((f32[256,1,512]{2,1,0:T(1,128)}), f32[256,1,512]{2,1,0:T(1,128)S(1)}, u32[]{:S(2)}, u32[]{:S(2)}) async-start(f32[256,1,512]{2,1,0:T(1,128)} %copy.51), calls=%async_computation.1 | async-start | bytes 1048576 | tf_op jit(solution)/shard_map/all_to_all | solution.py:119
  110.1 0.4 convolution_bitcast_fusion.4
  110.5 19.2 %all-to-all-done.1 = f32[256,1,512]{2,1,0:T(1,128)S(1)} async-done(((f32[256,1,512]{2,1,0:T(1,128)}), f32[256,1,512]{2,1,0:T(1,128)S(1)}, u32[]{:S(2)}, u32[]{:S(2)}) %all-to-all-start.1) | async-done | bytes 524320 | tf_op jit(solution)/shard_map/all_to_all | solution.py:119
  130.1 0.7 fusion.3
  130.7 1.2 pad_maximum_fusion
  131.9 14.8 %all-to-all-start.2 = ((f32[64,8,513]{2,1,0:T(8,128)}), f32[64,8,513]{2,1,0:T(8,128)S(1)}, u32[]{:S(2)}, u32[]{:S(2)}) async-start(f32[64,8,513]{2,1,0:T(8,128)} %pad_maximum_fusion), calls=%async_computation.2 | async-start | bytes 2621440 | tf_op jit(solution)/shard_map/all_to_all | solution.py:25
  146.7 34.2 %all-to-all-done.2 = f32[64,8,513]{2,1,0:T(8,128)S(1)} async-done(((f32[64,8,513]{2,1,0:T(8,128)}), f32[64,8,513]{2,1,0:T(8,128)S(1)}, u32[]{:S(2)}, u32[]{:S(2)}) %all-to-all-start.2) | async-done | bytes 1050656 | tf_op jit(solution)/shard_map/all_to_all | solution.py:25
  181.1 0.5 fusion
  181.6 0.7 fusion.31
  182.3 4.9 %all_to_all.73 = f32[32,2,8,512]{3,2,0,1:T(8,128)S(1)} all-to-all(f32[32,2,8,512]{3,2,0,1:T(8,128)S(1)} %copy.55), channel_id=1, replica_groups=mesh['grid_0'=8,'grid_1'=4,'grid_2'=2,'shard'=16] {'grid_2'}, dimensions={1} | all-to-all | bytes 2097152 | tf_op jit(solution)/shard_map/all_to_all | solution.py:51
  187.3 1.1 copy.56
  188.3 4.9 %all-to-all-start.4 = ((f32[32,2,8,512]{3,2,1,0:T(8,128)}), f32[32,2,8,512]{3,2,1,0:T(8,128)S(1)}, u32[]{:S(2)}, u32[]{:S(2)}) async-start(f32[32,2,8,512]{3,2,1,0:T(8,128)} %copy.56), calls=%async_computation.4 | async-start | bytes 2097152 | tf_op jit(solution)/shard_map/all_to_all | solution.py:51
  193.4 26.9 %all-to-all-done.4 = f32[32,2,8,512]{3,2,1,0:T(8,128)S(1)} async-done(((f32[32,2,8,512]{3,2,1,0:T(8,128)}), f32[32,2,8,512]{3,2,1,0:T(8,128)S(1)}, u32[]{:S(2)}, u32[]{:S(2)}) %all-to-all-start.4) | async-done | bytes 1048608 | tf_op jit(solution)/shard_map/all_to_all | solution.py:51
  220.3 0.7 fusion.158
  221.0 0.6 convolution_bitcast_fusion.1
  221.9 24.6 %all_to_all.74 = f32[16,16,512]{2,0,1:T(8,128)S(1)} all-to-all(f32[16,16,512]{2,0,1:T(8,128)S(1)} %copy.57), channel_id=1, replica_groups=mesh['grid_0'=8,'grid_1'=4,'grid_2'=2,'shard'=16] {'shard'}, dimensions={1} | all-to-all | bytes 1048576 | tf_op jit(solution)/shard_map/all_to_all | solution.py:116
  246.8 1.0 fusion.159
  247.9 1.9 convolution_bitcast_fusion
  249.8 0.5 copy.59
  250.3 24.0 %all_to_all.75 = f32[256,1,512]{2,1,0:T(1,128)S(1)} all-to-all(f32[256,1,512]{2,1,0:T(1,128)S(1)} %copy.59), channel_id=1, replica_groups=mesh['grid_0'=8,'grid_1'=4,'grid_2'=2,'shard'=16] {'shard'}, dimensions={0} | all-to-all | bytes 1048576 | tf_op jit(solution)/shard_map/all_to_all | solution.py:119
  274.3 1.1 copy.67
  (45 shorter events, 2.9 us)
Async XLA Ops:
  0.0 7.8 %copy-start = (f32[1,16,16,512]{3,2,1,0:T(8,128)S(1)}, f32[1,16,16,512]{3,2,1,0:T(8,128)}, u32[]{:S(2)}) copy-start(f32[1,16,16,512]{3,2,1,0:T(8,128)} %param.14) | copy-start | bytes 1572868
  0.0 45.7 %copy-start.6 = (f32[8,8]{1,0:T(8,128)S(1)}, f32[8,8]{1,0:T(8,128)}, u32[]{:S(2)}) copy-start(f32[8,8]{1,0:T(8,128)} %constant.329.clone) | copy-start | bytes 772
  0.0 45.9 %copy-start.7 = (f32[4,4]{1,0:T(4,128)S(1)}, f32[4,4]{1,0:T(4,128)}, u32[]{:S(2)}) copy-start(f32[4,4]{1,0:T(4,128)} %constant.330.clone) | copy-start | bytes 196
  9.5 85.7 %all-to-all-start = ((f32[16,16,512]{2,0,1:T(8,128)}), f32[16,16,512]{2,0,1:T(8,128)S(1)}, u32[]{:S(2)}, u32[]{:S(2)}) async-start(f32[16,16,512]{2,0,1:T(8,128)} %copy.50), calls=%async_computation | async-start | bytes 1048576 | tf_op jit(solution)/shard_map/all_to_all | solution.py:116
  46.5 2.0 copy-start.3
  63.0 31.4 %copy-start.5 = (f32[256,256]{1,0:T(8,128)S(1)}, f32[256,256]{1,0:T(8,128)}, u32[]{:S(2)}) copy-start(f32[256,256]{1,0:T(8,128)} %constant.327.clone) | copy-start | bytes 786436
  98.2 31.5 %all-to-all-start.1 = ((f32[256,1,512]{2,1,0:T(1,128)}), f32[256,1,512]{2,1,0:T(1,128)S(1)}, u32[]{:S(2)}, u32[]{:S(2)}) async-start(f32[256,1,512]{2,1,0:T(1,128)} %copy.51), calls=%async_computation.1 | async-start | bytes 1048576 | tf_op jit(solution)/shard_map/all_to_all | solution.py:119
  131.9 49.0 %all-to-all-start.2 = ((f32[64,8,513]{2,1,0:T(8,128)}), f32[64,8,513]{2,1,0:T(8,128)S(1)}, u32[]{:S(2)}, u32[]{:S(2)}) async-start(f32[64,8,513]{2,1,0:T(8,128)} %pad_maximum_fusion), calls=%async_computation.2 | async-start | bytes 2621440 | tf_op jit(solution)/shard_map/all_to_all | solution.py:25
  188.3 32.6 %copy-start.4 = (f32[16,16,1]{1,0,2:T(8,128)S(1)}, f32[16,16,1]{1,0,2:T(8,128)}, u32[]{:S(2)}) copy-start(f32[16,16,1]{1,0,2:T(8,128)} %constant.342) | copy-start | bytes 3076
  188.3 31.9 %all-to-all-start.4 = ((f32[32,2,8,512]{3,2,1,0:T(8,128)}), f32[32,2,8,512]{3,2,1,0:T(8,128)S(1)}, u32[]{:S(2)}, u32[]{:S(2)}) async-start(f32[32,2,8,512]{3,2,1,0:T(8,128)} %copy.56), calls=%async_computation.4 | async-start | bytes 2097152 | tf_op jit(solution)/shard_map/all_to_all | solution.py:51
  220.9 25.9 %copy-start.2 = (f32[256,256]{1,0:T(8,128)S(1)}, f32[256,256]{1,0:T(8,128)}, u32[]{:S(2)}) copy-start(f32[256,256]{1,0:T(8,128)} %constant.341) | copy-start | bytes 786436
  221.5 26.3 %copy-start.1 = (f32[512,512]{1,0:T(8,128)S(1)}, f32[512,512]{1,0:T(8,128)}, u32[]{:S(2)}) copy-start(f32[512,512]{1,0:T(8,128)} %constant.333.clone) | copy-start | bytes 3145732
where the time goes:
time: 278 us; the launch traced here: 275 us
  waiting for transfers between devices  80.3 us (29%)
  blocking collectives  53.5 us (19%)
  starting transfers between devices  51.4 us (18%)
  local copies, waits for them, and re-layouts  40.3 us (14%)
  other arithmetic  21.4 us (8%)
  between operations  17.3 us (6%)
  matrix products  11.1 us (4%)
    all_to_all x1, waiting for transfers between devices, side_by_side(): lax.all_to_all(both, axis, split_axis=split_dim, concat_axis=concat_dim,...  34.2 us
    mul x3, local copies, waits for them, and re-layouts, kron_pair(): return jnp.kron(left_matrix, right_matrix)  30.5 us
    all_to_all x1, waiting for transfers between devices, exchange_in_order(): lax.all_to_all(pieces, axes[k], split_axis=k, concat_axis=k, tiled=True)  26.9 us
    all_to_all x1, blocking collectives, transform(): lax.all_to_all(volume, 'shard', split_axis=1, concat_axis=0, tiled=True)  24.6 us
    all_to_all x1, blocking collectives, transform(): lax.all_to_all(pencil, 'shard', split_axis=0, concat_axis=1, tiled=True)  24 us
    all_to_all x1, starting transfers between devices, transform(): lax.all_to_all(volume, 'shard', split_axis=1, concat_axis=0, tiled=True)  20.3 us
    all_to_all x1, waiting for transfers between devices, transform(): lax.all_to_all(pencil, 'shard', split_axis=0, concat_axis=1, tiled=True)  19.2 us
    all_to_all x1, starting transfers between devices, side_by_side(): lax.all_to_all(both, axis, split_axis=split_dim, concat_axis=concat_dim,...  14.8 us
  transfers between devices with their start and end apart: 4, of which 3 were waited for; matrix products, arithmetic and copies ran while one was open for 19% of the time, Pallas kernels for 0%

commit v1 on v0

v1 whole, which is shorter than its diff:
```python
import functools

import jax
import jax.numpy as jnp
import numpy as np
from jax import lax
from jax.experimental import pallas as pl
from jax.experimental.pallas import tpu as pltpu
from jax.sharding import PartitionSpec as P

MESH = pl.DeviceIdType.MESH
CORES = 2
GROUP = 32
LANES = 128
TAIL_DIMS = (8, 4, 4, 4)
IDS = 1024

f32 = jnp.float32
bf16 = jnp.bfloat16


def dehier_table(length):
    matrix = np.eye(length)
    for level_index in reversed(range(length.bit_length() - 1)):
        spacing = 2**level_index
        for position in range(spacing, length, 2 * spacing):
            matrix[position] = matrix[position] + 0.5 * (
                matrix[position - spacing] + matrix[(position + spacing) % length]
            )
    return matrix


def iota(shape, dim):
    return lax.broadcasted_iota(jnp.int32, shape, dim)


def split(value):
    high = value.astype(bf16)
    return high, (value - high.astype(f32)).astype(bf16)


def dot(left, right):
    return jnp.dot(left, right, preferred_element_type=f32)


def dot_t(left, right):
    return lax.dot_general(left, right, (((1,), (1,)), ((), ())), preferred_element_type=f32)


def stencil_weights(fraction):
    r = 1.0 - fraction
    sixth = 1.0 / 6.0
    return (
        -r * (r - 1.0) * (r - 2.0) * sixth,
        (r + 1.0) * (r - 1.0) * (r - 2.0) * 0.5,
        -(r + 1.0) * r * (r - 2.0) * 0.5,
        (r + 1.0) * r * (r - 1.0) * sixth,
    )


def sweep(row, col, length, shift, weights):
    step = (col - row + (shift + 2)) & (length - 1)
    out = jnp.where(step == 3, weights[3], 0.0)
    for k in range(3):
        out = jnp.where(step == k, weights[k], out)
    return out


def forward_entry(row, col, length, shift, weights):
    low = row & (-row)
    here = sweep(row, col, length, shift, weights)
    sides = sweep(row - low, col, length, shift, weights) + sweep(
        row + low, col, length, shift, weights
    )
    return jnp.where(row == 0, here, here - 0.5 * sides)


def swap_groups(tiles):
    lane = iota(tiles[0].shape, 1)
    low64 = lane < 64
    even32 = (lane & 32) == 0
    half = [None] * 4
    for a in (0, 1):
        b = a + 2
        half[a] = jnp.where(low64, tiles[a], pltpu.roll(tiles[b], 64, 1))
        half[b] = jnp.where(low64, pltpu.roll(tiles[a], 64, 1), tiles[b])
    done = [None] * 4
    for a in (0, 2):
        b = a + 1
        done[a] = jnp.where(even32, half[a], pltpu.roll(half[b], 32, 1))
        done[b] = jnp.where(even32, pltpu.roll(half[a], 96, 1), half[b])
    return done


def spread_groups(value):
    value = value + pltpu.roll(value, 64, 1)
    return value + pltpu.roll(value, 32, 1)


def step_kernel(
    cfg,
    coef,
    shifts,
    fracs,
    x_ref,
    ids_ref,
    dlead_hbm,
    dsecond_hbm,
    dtail_hbm,
    out_ref,
    dlead,
    dsecond,
    dtail,
    chi,
    clo,
    pxs,
    thi,
    tlo,
    lhi,
    llo,
    vbuf,
    wbuf,
    rbuf,
    fbuf,
    gbuf,
    idown,
    idall,
    idmine,
    idrow,
    hot,
    hot_t,
    rhs,
    acc,
    table,
    zrecv,
    zsum,
    tsum,
    tsplit,
    abuf,
    bbuf,
    obuf,
    ubuf,
    const_sem,
    id_send,
    id_recv,
    send_sem,
    recv_sem,
    z_send,
    z_recv,
):
    S, ZN, AL, BN, NQ = cfg.shards, cfg.zs, cfg.rows, cfg.second, cfg.chunks
    A, TAIL = cfg.lead, cfg.tail
    ROWS = AL * BN
    g = lax.axis_index("grid")
    s = lax.axis_index("shard")
    core = lax.rem(g, CORES)
    zz = lax.rem(g // CORES, ZN)
    xx = g // (CORES * ZN)
    own = xx * CORES + core

    def owner_grid(o):
        return ((o // CORES) * ZN + zz) * CORES + lax.rem(o, CORES)

    def z_grid(z):
        return (xx * ZN + z) * CORES + core

    barrier = pltpu.get_barrier_semaphore()

    def greet(k, carry):
        pl.semaphore_signal(
            barrier, inc=1, device_id=(g, lax.rem(s + k, S)), device_id_type=MESH
        )
        pl.semaphore_signal(
            barrier, inc=1, device_id=(owner_grid(lax.rem(own + k, S)), s), device_id_type=MESH
        )
        return carry

    lax.fori_loop(1, S, greet, 0)

    def greet_z(k, carry):
        pl.semaphore_signal(
            barrier, inc=1, device_id=(z_grid(lax.rem(zz + k, ZN)), s), device_id_type=MESH
        )
        return carry

    lax.fori_loop(1, ZN, greet_z, 0)

    consts = [
        pltpu.make_async_copy(dlead_hbm, dlead, const_sem.at[0]),
        pltpu.make_async_copy(dsecond_hbm, dsecond, const_sem.at[1]),
        pltpu.make_async_copy(dtail_hbm, dtail, const_sem.at[2]),
    ]
    for copy in consts:
        copy.start()

    weights = [stencil_weights(fracs[0, d]) for d in range(6)]
    shift = [shifts[0, d] for d in range(6)]

    idown[...] = jnp.zeros_like(idown)
    idown[:, 0:BN] = ids_ref[...].astype(f32)

    RB = 32

    def build_second(i, carry):
        row = iota((RB, ROWS), 0) + i * RB
        col = iota((RB, ROWS), 1)
        entry = forward_entry(row // AL, col & (BN - 1), BN, shift[1], weights[1])
        entry = jnp.where((row & (AL - 1)) == col // BN, entry, 0.0)
        high, low = split(entry)
        chi[pl.ds(i * RB, RB), :] = high
        clo[pl.ds(i * RB, RB), :] = low
        return carry

    lax.fori_loop(0, ROWS // RB, build_second, 0)

    n2, n3, n4, n5 = cfg.tail_dims
    PN, QN = n2 * n3, n4 * n5
    prow, pcol = iota((PN, TAIL), 0), iota((PN, TAIL), 1) // QN
    first = forward_entry(prow // n3, pcol // n3, n2, shift[2], weights[2])
    if n3 > 1:
        first = first * forward_entry(
            prow & (n3 - 1), pcol & (n3 - 1), n3, shift[3], weights[3]
        )
    pxs[...] = first
    qrow, qcol = iota((QN, TAIL), 0), iota((QN, TAIL), 1) & (QN - 1)
    last = forward_entry(qrow // n5, qcol // n5, n4, shift[4], weights[4]) * forward_entry(
        qrow & (n5 - 1), qcol & (n5 - 1), n5, shift[5], weights[5]
    )

    def build_tail(i, carry):
        high, low = split(pxs[pl.ds(i, 1), :] * last)
        thi[pl.ds(i * QN, QN), :] = high
        tlo[pl.ds(i * QN, QN), :] = low
        return carry

    lax.fori_loop(0, PN, build_tail, 0)

    xh, xl = split(x_ref[...])
    u = dot(chi[...], xh) + dot(chi[...], xl) + dot(clo[...], xh)
    uh, ul = split(u)
    vbuf[...] = dot_t(uh, thi[...]) + dot_t(uh, tlo[...]) + dot_t(ul, thi[...])

    PG = TAIL // LANES
    for q in range(NQ):
        for p in range(PG):
            tiles = [
                vbuf[pl.ds((4 * q + j) * AL, AL), pl.ds(p * LANES, LANES)] for j in range(4)
            ]
            for i, tile in enumerate(swap_groups(tiles)):
                wbuf[q, 4 * p + i] = tile

    pl.semaphore_wait(barrier, 2 * (S - 1) + (ZN - 1))

    def send_ids(k, carry):
        to = lax.rem(s + k, S)
        pltpu.make_async_remote_copy(
            idown,
            idall.at[s],
            id_send.at[0],
            id_recv.at[0],
            device_id=(g, to),
            device_id_type=MESH,
        ).start()
        return carry

    lax.fori_loop(1, S, send_ids, 0)

    def send_to_shards(src, dst_of, phase, q):
        def body(k, carry):
            to = lax.rem(s + k, S)
            pltpu.make_async_remote_copy(
                src(to),
                dst_of,
                send_sem.at[phase, q],
                recv_sem.at[phase, q],
                device_id=(g, to),
                device_id_type=MESH,
            ).start()
            return carry

        lax.fori_loop(1, S, body, 0)

    def send_to_owners(src, dst_of, phase, q):
        def body(k, carry):
            to = lax.rem(own + k, S)
            pltpu.make_async_remote_copy(
                src(to),
                dst_of,
                send_sem.at[phase, q],
                recv_sem.at[phase, q],
                device_id=(owner_grid(to), s),
                device_id_type=MESH,
            ).start()
            return carry

        lax.fori_loop(1, S, body, 0)

    def all_bytes(ref, sem):
        pltpu.make_async_copy(ref, ref, sem).wait()

    peers = pl.ds(0, S - 1)

    for q in range(NQ):
        send_to_shards(lambda to: wbuf.at[q, to], rbuf.at[q, s], 0, q)
        rbuf[q, pl.ds(s, 1)] = wbuf[q, pl.ds(s, 1)]

    scale = coef[0].astype(f32)
    scaled = [w * scale for w in weights[0]]

    def build_lead(i, carry):
        row = iota((RB, A), 0) + i * RB
        col = iota((RB, A), 1)
        high, low = split(forward_entry(row, col, A, shift[0], scaled))
        lhi[pl.ds(i * RB, RB), :] = high
        llo[pl.ds(i * RB, RB), :] = low
        return carry

    lax.fori_loop(0, A // RB, build_lead, 0)

    idall[pl.ds(s, 1)] = idown[...][None]
    all_bytes(idall.at[peers], id_recv.at[0])

    def send_ids_on(k, carry):
        to = lax.rem(own + k, S)
        pltpu.make_async_remote_copy(
            idall.at[to],
            idmine.at[own],
            id_send.at[1],
            id_recv.at[1],
            device_id=(owner_grid(to), s),
            device_id_type=MESH,
        ).start()
        return carry

    lax.fori_loop(1, S, send_ids_on, 0)
    idmine[pl.ds(own, 1)] = idall[pl.ds(own, 1)]

    GA = S * AL
    NG = cfg.ids

    def build_hot(q):
        for j in range(4):
            b = 4 * q + j
            ids_here = idrow[b : b + 1, :]
            column = idmine[...].reshape(GA, LANES)[:, b : b + 1].astype(jnp.int32)

            def rows(i, carry):
                number = iota((RB, GA), 0) + i * RB
                hot[q, pl.ds(i * RB, RB), j * GA : (j + 1) * GA] = jnp.where(
                    number == ids_here, 1.0, 0.0
                ).astype(bf16)
                return carry

            lax.fori_loop(0, NG // RB, rows, 0)
            for i in range(GA // RB):
                hot_t[q, j * GA + i * RB : j * GA + (i + 1) * RB, :] = jnp.where(
                    iota((RB, NG), 1) == column[i * RB : (i + 1) * RB], 1.0, 0.0
                ).astype(bf16)

    lane_group = iota((1, LANES), 1) // GROUP

    for q in range(NQ):
        all_bytes(rbuf.at[q, peers], recv_sem.at[0, q])
        rh, rl = split(rbuf[q].reshape(A, LANES))
        fbuf[q] = (dot(lhi[...], rh) + dot(lhi[...], rl) + dot(llo[...], rh)).reshape(
            S, AL, LANES
        )
        send_to_owners(lambda to: fbuf.at[q, to], gbuf.at[q, own], 1, q)
        gbuf[q, pl.ds(own, 1)] = fbuf[q, pl.ds(own, 1)]
        if q == 0:
            all_bytes(idmine.at[peers], id_recv.at[1])
            idrow[...] = jnp.transpose(idmine[...].reshape(GA, LANES)).astype(jnp.int32)
        build_hot(q)

    acc[...] = jnp.zeros_like(acc)

    for q in range(NQ):
        all_bytes(gbuf.at[q, peers], recv_sem.at[1, q])
        value = gbuf[q].reshape(GA, LANES)
        high = value.astype(bf16).astype(f32)
        low = value - high
        for j in range(4):
            here = lane_group == j
            rhs[j * GA : (j + 1) * GA, 0:LANES] = jnp.where(here, high, 0.0).astype(bf16)
            rhs[j * GA : (j + 1) * GA, LANES:] = jnp.where(here, low, 0.0).astype(bf16)
        acc[...] += dot(hot[q], rhs[...])

    QI = NG // 4
    packed = jnp.zeros((QI, LANES), f32)
    for k in range(4):
        part = acc[k * QI : (k + 1) * QI, :]
        packed = jnp.where(
            lane_group == k, spread_groups(part[:, :LANES] + part[:, LANES:]), packed
        )
    ZR = QI // ZN
    table[...] = packed.reshape(ZN, ZR, LANES)

    def send_z(k, carry):
        to = lax.rem(zz + k, ZN)
        pltpu.make_async_remote_copy(
            table.at[to],
            zrecv.at[zz],
            z_send.at[0],
            z_recv.at[0],
            device_id=(z_grid(to), s),
            device_id_type=MESH,
        ).start()
        return carry

    lax.fori_loop(1, ZN, send_z, 0)
    zrecv[pl.ds(zz, 1)] = table[pl.ds(zz, 1)]
    zpeers = pl.ds(0, ZN - 1)
    all_bytes(zrecv.at[zpeers], z_recv.at[0])
    total = zrecv[0]
    for k in range(1, ZN):
        total = total + zrecv[k]
    zsum[...] = total

    def send_sum(k, carry):
        to = lax.rem(zz + k, ZN)
        pltpu.make_async_remote_copy(
            zsum,
            tsum.at[zz],
            z_send.at[1],
            z_recv.at[1],
            device_id=(z_grid(to), s),
            device_id_type=MESH,
        ).start()
        return carry

    lax.fori_loop(1, ZN, send_sum, 0)
    tsum[pl.ds(zz, 1)] = total[None]
    all_bytes(tsum.at[zpeers], z_recv.at[1])
    packed = tsum[...].reshape(QI, LANES)
    for k in range(4):
        high, low = split(spread_groups(jnp.where(lane_group == k, packed, 0.0)))
        tsplit[k * QI : (k + 1) * QI, 0:LANES] = high
        tsplit[k * QI : (k + 1) * QI, LANES:] = low

    for q in range(NQ):
        answer = jnp.zeros((GA, LANES), f32)
        for j in range(4):
            rows_j = dot(hot_t[q, j * GA : (j + 1) * GA, :], tsplit[...])
            answer = jnp.where(lane_group == j, rows_j[:, :LANES] + rows_j[:, LANES:], answer)
        abuf[q] = answer.reshape(S, AL, LANES)
        send_to_owners(lambda to: abuf.at[q, to], bbuf.at[q, own], 2, q)
        bbuf[q, pl.ds(own, 1)] = abuf[q, pl.ds(own, 1)]

    for copy in consts:
        copy.wait()

    for q in range(NQ):
        all_bytes(bbuf.at[q, peers], recv_sem.at[2, q])
        bh, bl = split(bbuf[q].reshape(A, LANES))
        obuf[q] = (dot(dlead[...], bh) + dot(dlead[...], bl)).reshape(S, AL, LANES)
        send_to_shards(lambda to: obuf.at[q, to], ubuf.at[q, s], 3, q)
        ubuf[q, pl.ds(s, 1)] = obuf[q, pl.ds(s, 1)]

    for q in range(NQ):
        all_bytes(ubuf.at[q, peers], recv_sem.at[3, q])
        for p in range(PG):
            for j, tile in enumerate(swap_groups([ubuf[q, 4 * p + i] for i in range(4)])):
                vbuf[pl.ds((4 * q + j) * AL, AL), pl.ds(p * LANES, LANES)] = tile

    vh, vl = split(vbuf[...])
    y = dot_t(vh, dtail[...]) + dot_t(vl, dtail[...])
    yh, yl = split(y)
    out_ref[...] = dot(dsecond[...], yh) + dot(dsecond[...], yl)

    all_bytes(idall.at[peers], id_send.at[0])
    all_bytes(idall.at[peers], id_send.at[1])
    all_bytes(table.at[zpeers], z_send.at[0])
    all_bytes(tsum.at[zpeers], z_send.at[1])
    for phase in range(4):
        for q in range(NQ):
            all_bytes(wbuf.at[q, peers], send_sem.at[phase, q])


class Config:
    pass


def run_step(cfg, x, coef, shifts, fracs, ids):
    S, ZN, AL, BN, NQ = cfg.shards, cfg.zs, cfg.rows, cfg.second, cfg.chunks
    A, TAIL, NG = cfg.lead, cfg.tail, cfg.ids
    GA, ROWS, QI = S * AL, AL * BN, NG // 4
    n2, n3, n4, n5 = cfg.tail_dims
    dlead = jnp.asarray(dehier_table(A), bf16)
    second = np.einsum("bc,ad->abcd", dehier_table(BN), np.eye(AL)).reshape(ROWS, ROWS)
    dsecond = jnp.asarray(second, bf16)
    dtail = jnp.asarray(
        functools.reduce(np.kron, [dehier_table(n) for n in cfg.tail_dims]), bf16
    )
    vmem, smem = pl.BlockSpec(memory_space=pltpu.VMEM), pl.BlockSpec(memory_space=pltpu.SMEM)
    hbm = pl.BlockSpec(memory_space=pl.ANY)
    V, D = pltpu.VMEM, pltpu.SemaphoreType.DMA
    slabs = V((NQ, S, AL, LANES), f32)
    return pl.pallas_call(
        functools.partial(step_kernel, cfg),
        out_shape=jax.ShapeDtypeStruct((ROWS, TAIL), f32),
        in_specs=[smem, smem, smem, vmem, vmem, hbm, hbm, hbm],
        out_specs=vmem,
        scratch_shapes=[
            V((A, A), bf16),
            V((ROWS, ROWS), bf16),
            V((TAIL, TAIL), bf16),
            V((ROWS, ROWS), bf16),
            V((ROWS, ROWS), bf16),
            V((n2 * n3, TAIL), f32),
            V((TAIL, TAIL), bf16),
            V((TAIL, TAIL), bf16),
            V((A, A), bf16),
            V((A, A), bf16),
            V((ROWS, TAIL), f32),
            slabs,
            slabs,
            slabs,
            slabs,
            V((AL, LANES), f32),
            V((S, AL, LANES), f32),
            V((S, AL, LANES), f32),
            V((LANES, GA), jnp.int32),
            V((NQ, NG, 4 * GA), bf16),
            V((NQ, 4 * GA, NG), bf16),
            V((4 * GA, 2 * LANES), bf16),
            V((NG, 2 * LANES), f32),
            V((ZN, QI // ZN, LANES), f32),
            V((ZN, QI // ZN, LANES), f32),
            V((QI // ZN, LANES), f32),
            V((ZN, QI // ZN, LANES), f32),
            V((NG, 2 * LANES), bf16),
            slabs,
            slabs,
            slabs,
            slabs,
            D((3,)),
            D((2,)),
            D((2,)),
            D((4, NQ)),
            D((4, NQ)),
            D((2,)),
            D((2,)),
        ],
        compiler_params=pltpu.CompilerParams(
            collective_id=0, has_side_effects=True, vmem_limit_bytes=60 * 1024 * 1024
        ),
    )(coef, shifts, fracs, x, ids, dlead, dsecond, dtail)


def build(mesh, tail_dims, id_count):
    def body(density, coefficients, offsets, fractions, subspace_ids):
        _, rows, second, tail = density.shape
        cfg = Config()
        cfg.shards = mesh.shape["shard"]
        cfg.zs = mesh.shape["grid"] // cfg.shards
        cfg.rows, cfg.second, cfg.tail = rows, second, tail
        cfg.lead = rows * cfg.shards
        cfg.chunks = second * GROUP // LANES
        cfg.tail_dims, cfg.ids = tail_dims, id_count
        out = run_step(
            cfg,
            density.reshape(rows * second, tail),
            coefficients,
            offsets,
            fractions,
            subspace_ids[0],
        )
        return out.reshape(density.shape)

    return jax.shard_map(
        body,
        mesh=mesh,
        in_specs=(
            P("grid", "shard", None, None),
            P("grid"),
            P("grid", None),
            P("grid", None),
            P("grid", "shard", None),
        ),
        out_specs=P("grid", "shard", None, None),
        check_vma=False,
    )


def solution(mesh):
    return build(mesh, TAIL_DIMS, IDS)
```

time: 278 us -> 98.1 us (0.35)
  Pallas kernels: 0 us -> 95.3 us
  waiting for transfers between devices: 80.3 us -> 0 us
  blocking collectives: 53.5 us -> 0 us
  starting transfers between devices: 51.4 us -> 0 us
  local copies, waits for them, and re-layouts: 40.3 us -> 1.88 us
  other arithmetic: 21.4 us -> 0 us
  between operations: 17.3 us -> 0.66 us
  matrix products: 11.1 us -> 0 us
    pallas_call x0 -> x1, Pallas kernels: none -> 95.3 us  [run_step(): pl.pallas_call(functools.partial(step_kernel, cfg), out_shape=jax.ShapeDt...]
    all_to_all x4 -> x0, waiting for transfers between devices: 80.3 us -> none  [the longest x1 34.2 us: side_by_side(): lax.all_to_all(both, axis, split_axis=split_dim, concat_axis=concat_dim,...]
    all_to_all x3 -> x0, blocking collectives: 53.5 us -> none  [the longest x1 24.6 us: transform(): lax.all_to_all(volume, 'shard', split_axis=1, concat_axis=0, tiled=True)]
    all_to_all x4 -> x0, starting transfers between devices: 51.4 us -> none  [the longest x1 20.3 us: transform(): lax.all_to_all(volume, 'shard', split_axis=1, concat_axis=0, tiled=True)]
    mul x4 -> x0, local copies, waits for them, and re-layouts: 30.8 us -> none  [the longest x3 30.5 us: kron_pair(): return jnp.kron(left_matrix, right_matrix)]
    mul x4 -> x0, other arithmetic: 11.8 us -> none  [the longest x3 11.8 us: kron_pair(): return jnp.kron(left_matrix, right_matrix)]
    dot_general x17 -> x0, matrix products: 11.1 us -> none  [the longest x2 2.92 us: apply_tail(): return jnp.einsum('abx,tx->abt', volume, tail_matrix, precision=highest)]
    select_n x14 -> x0, other arithmetic: 7.53 us -> none  [the longest x12 7.51 us: sweep_matrix(): source = jnp.mod(row_index - shift - 2 + stencil, length)]
  transfers between devices with their start and end apart: 4 -> 0, of which waited for: 3 -> 0; matrix products, arithmetic and copies ran while one was open for 19% -> 0% of each run, Pallas kernels for 0% -> 0%
where the time goes in v1:
time: 98.1 us; the launch traced here: 97.9 us
  Pallas kernels  95.3 us (97%)
  local copies, waits for them, and re-layouts  1.88 us (2%)
    pallas_call x1, Pallas kernels, run_step(): pl.pallas_call(functools.partial(step_kernel, cfg), out_shape=jax.ShapeDt...  95.3 us

profile of v1, /device:TPU:1, one launch (start us, length us, event | category | flops | bytes accessed | tf_op | source)
XLA Modules:
  0.0 97.9 jit_solution(4272174917831333589)
XLA Ops:
  0.7 95.3 %shard_map.82 = f32[256,512]{1,0:T(8,128)} custom-call(s32[1]{0:T(128)S(6)} %copy.10.coef, s32[1,6]{1,0:T(1,128)} %shifts.1, f32[1,6]{1,0:T(1,128)} %fracs.1, f32[256,512]{1,0:T(8,128)} %bitcast.4, s32[16,16]{1,0:T(8,128)} %bitcast.5, bf16[256,256]{1,0:T(8,128)(2,1)} %constant.6.clone.dlead_hbm, bf16[256,256]{1,0:T(8,128)(2,1)} %constant.7.clone.dsecond_hbm, ...), custom_call_target="tpu_custom_call" | custom-call | tf_op jit(solution)/shard_map/pallas_call | solution.py:498
  96.0 1.9 %copy.11 = f32[1,16,16,512]{3,2,1,0:T(8,128)} copy(f32[1,16,16,512]{3,2,1,0:T(8,128)} %bitcast.3) | data formatting | bytes 1048576

commit v2 on v1

v2 whole, which is shorter than its diff:
```python
import functools

import jax
import jax.numpy as jnp
from jax import lax
from jax.experimental import pallas as pl
from jax.experimental.pallas import tpu as pltpu
from jax.sharding import PartitionSpec as P

MESH = pl.DeviceIdType.MESH
CORES = 2
GROUP = 32
LANES = 128
TAIL_DIMS = (8, 4, 4, 4)
IDS = 1024
PACK = 8
PARTS = 1

f32 = jnp.float32
bf16 = jnp.bfloat16


def iota(shape, dim):
    return lax.broadcasted_iota(jnp.int32, shape, dim)


def split(value):
    high = value.astype(bf16)
    return high, (value - high.astype(f32)).astype(bf16)


def dot(left, right):
    return jnp.dot(left, right, preferred_element_type=f32)


def dot_t(left, right):
    return lax.dot_general(left, right, (((1,), (1,)), ((), ())), preferred_element_type=f32)


def stencil_weights(fraction):
    r = 1.0 - fraction
    sixth = 1.0 / 6.0
    return (
        -r * (r - 1.0) * (r - 2.0) * sixth,
        (r + 1.0) * (r - 1.0) * (r - 2.0) * 0.5,
        -(r + 1.0) * r * (r - 2.0) * 0.5,
        (r + 1.0) * r * (r - 1.0) * sixth,
    )


def sweep(row, col, length, shift, weights):
    step = (col - row + (shift + 2)) & (length - 1)
    out = jnp.where(step == 3, weights[3], 0.0)
    for k in range(3):
        out = jnp.where(step == k, weights[k], out)
    return out


def forward_entry(row, col, length, shift, weights):
    low = row & (-row)
    here = sweep(row, col, length, shift, weights)
    sides = sweep(row - low, col, length, shift, weights) + sweep(
        row + low, col, length, shift, weights
    )
    return jnp.where(row == 0, here, here - 0.5 * sides)


def backward_entry(row, col):
    width = (col & (-col)).astype(f32)
    away = jnp.abs(row - col).astype(f32)
    hat = jnp.maximum(width - away, 0.0) / jnp.where(col == 0, 1.0, width)
    return jnp.where(col == 0, 1.0, hat)


def swap_groups(tiles):
    lane = iota(tiles[0].shape, 1)
    low64 = lane < 64
    even32 = (lane & 32) == 0
    half = [None] * 4
    for a in (0, 1):
        b = a + 2
        half[a] = jnp.where(low64, tiles[a], pltpu.roll(tiles[b], 64, 1))
        half[b] = jnp.where(low64, pltpu.roll(tiles[a], 64, 1), tiles[b])
    done = [None] * 4
    for a in (0, 2):
        b = a + 1
        done[a] = jnp.where(even32, half[a], pltpu.roll(half[b], 32, 1))
        done[b] = jnp.where(even32, pltpu.roll(half[a], 96, 1), half[b])
    return done


def step_kernel(
    cfg,
    coef_hbm,
    shifts_hbm,
    fracs_hbm,
    x_hbm,
    ids_hbm,
    out_ref,
    coef,
    shifts,
    fracs,
    ids_ref,
    xbuf,
    dlead,
    dsecond,
    dtail,
    chi,
    clo,
    pxs,
    thi,
    tlo,
    lhi,
    llo,
    vbuf,
    wbuf,
    rbuf,
    fbuf,
    gbuf,
    idwide,
    idown,
    idall,
    idmine,
    idcol,
    idrow,
    quarter,
    hot,
    hot_t,
    rhs,
    acc,
    table,
    zrecv,
    zsum,
    tsum,
    tsplit,
    abuf,
    bbuf,
    obuf,
    ubuf,
    x_sem,
    id_send,
    id_recv,
    send_sem,
    recv_sem,
    z_send,
    z_recv,
):
    S, ZN, AL, BN, NQ = cfg.shards, cfg.zs, cfg.rows, cfg.second, cfg.chunks
    A, TAIL = cfg.lead, cfg.tail
    ROWS = AL * BN
    AH, NG = PARTS, cfg.ids
    RA, BQ, QI = AL // AH, 4 // AH, NG // 4
    GR = S * RA
    g = lax.axis_index("grid")
    s = lax.axis_index("shard")
    core = lax.rem(g, CORES)
    zz = lax.rem(g // CORES, ZN)
    xx = g // (CORES * ZN)
    own = xx * CORES + core

    def owner_grid(o):
        return ((o // CORES) * ZN + zz) * CORES + lax.rem(o, CORES)

    def z_grid(z):
        return (xx * ZN + z) * CORES + core

    copies = [
        pltpu.make_async_copy(src, dst, x_sem.at[k])
        for k, (src, dst) in enumerate(
            [
                (ids_hbm, ids_ref),
                (shifts_hbm, shifts),
                (fracs_hbm, fracs),
                (x_hbm, xbuf),
                (coef_hbm, coef),
            ]
        )
    ]
    for copy in copies:
        copy.start()
    barrier = pltpu.get_barrier_semaphore()

    def far_first(me, send):
        ring = S // 2
        u, v = me // 2, lax.rem(me, 2)

        def body(i, carry):
            sign = 1 - 2 * lax.rem(i, 2)
            step = ring // 2 + sign * ((i + 1) // 2)
            to = lax.rem(u + step + ring, ring) * 2
            send(to + 1 - v)
            send(to + v)
            return carry

        lax.fori_loop(0, ring - 1, body, 0)
        send(u * 2 + 1 - v)

    def greet(grid, shard):
        pl.semaphore_signal(barrier, inc=1, device_id=(grid, shard), device_id_type=MESH)

    far_first(s, lambda to: greet(g, to))
    far_first(own, lambda to: greet(owner_grid(to), s))

    def greet_z(k, carry):
        greet(z_grid(lax.rem(zz + k, ZN)), s)
        return carry

    lax.fori_loop(1, ZN, greet_z, 0)
    copies[0].wait()
    copies[1].wait()
    copies[2].wait()
    weights = [stencil_weights(fracs[0, d]) for d in range(6)]
    shift = [shifts[0, d] for d in range(6)]

    idwide[...] = jnp.zeros_like(idwide)
    idwide[:, 0:BN] = ids_ref[...].astype(f32)
    wide = idwide[...]
    for step in (BN, 2 * BN, 4 * BN):
        wide = wide + pltpu.roll(wide, step, 1)
    mine = (iota((AL, LANES), 1) // BN) == (iota((AL, LANES), 0) & (PACK - 1))
    wide = jnp.where(mine, wide, 0.0)
    for k in range(AL // PACK):
        idown[k : k + 1, :] = jnp.sum(
            wide[k * PACK : (k + 1) * PACK], axis=0, keepdims=True
        )

    RB = 32
    cells = forward_entry(
        iota((BN, ROWS), 0), iota((BN, ROWS), 1) & (BN - 1), BN, shift[1], weights[1]
    )
    own_row = iota((AL, ROWS), 0) == iota((AL, ROWS), 1) // BN
    for b in range(BN):
        high, low = split(jnp.where(own_row, cells[b : b + 1], 0.0))
        chi[b * AL : (b + 1) * AL, :] = high
        clo[b * AL : (b + 1) * AL, :] = low

    n2, n3, n4, n5 = cfg.tail_dims
    PN, QN = n2 * n3, n4 * n5
    prow, pcol = iota((PN, TAIL), 0), iota((PN, TAIL), 1) // QN
    first = forward_entry(prow // n3, pcol // n3, n2, shift[2], weights[2])
    if n3 > 1:
        first = first * forward_entry(
            prow & (n3 - 1), pcol & (n3 - 1), n3, shift[3], weights[3]
        )
    pxs[...] = first
    qrow, qcol = iota((QN, TAIL), 0), iota((QN, TAIL), 1) & (QN - 1)
    last = forward_entry(qrow // n5, qcol // n5, n4, shift[4], weights[4]) * forward_entry(
        qrow & (n5 - 1), qcol & (n5 - 1), n5, shift[5], weights[5]
    )

    def build_tail(i, carry):
        high, low = split(pxs[pl.ds(i, 1), :] * last)
        thi[pl.ds(i * QN, QN), :] = high
        tlo[pl.ds(i * QN, QN), :] = low
        return carry

    lax.fori_loop(0, PN, build_tail, 0)

    copies[3].wait()
    copies[4].wait()
    xh, xl = split(xbuf[...])
    u = dot(chi[...], xh) + dot(chi[...], xl) + dot(clo[...], xh)
    uh, ul = split(u)
    vbuf[...] = dot_t(uh, thi[...]) + dot_t(uh, tlo[...]) + dot_t(ul, thi[...])

    pl.semaphore_wait(barrier, 2 * (S - 1) + (ZN - 1))

    def to_shard(src, dst, send_at, recv_at):
        def send(to):
            pltpu.make_async_remote_copy(
                src(to), dst, send_at, recv_at, device_id=(g, to), device_id_type=MESH
            ).start()

        far_first(s, send)

    def to_owner(src, dst, send_at, recv_at):
        def send(to):
            pltpu.make_async_remote_copy(
                src(to),
                dst,
                send_at,
                recv_at,
                device_id=(owner_grid(to), s),
                device_id_type=MESH,
            ).start()

        far_first(own, send)

    to_shard(lambda to: idown, idall.at[s], id_send.at[0], id_recv.at[0])

    def send_to_shards(src, dst, phase, q):
        to_shard(src, dst, send_sem.at[phase, q], recv_sem.at[phase, q])

    def send_to_owners(src, dst, phase, q):
        to_owner(src, dst, send_sem.at[phase, q], recv_sem.at[phase, q])

    def all_bytes(ref, sem):
        pltpu.make_async_copy(ref, ref, sem).wait()

    peers = pl.ds(0, S - 1)

    PG = TAIL // LANES

    def group_row(q, j):
        return (q * BQ + j % BQ) * AL + j // BQ * RA

    for q in range(NQ):
        for p in range(PG):
            tiles = [
                vbuf[pl.ds(group_row(q, j), RA), pl.ds(p * LANES, LANES)] for j in range(4)
            ]
            for i, tile in enumerate(swap_groups(tiles)):
                wbuf[q, 4 * p + i] = tile
        send_to_shards(lambda to: wbuf.at[q, to], rbuf.at[q, s], 0, q)
        rbuf[q, pl.ds(s, 1)] = wbuf[q, pl.ds(s, 1)]

    scale = coef[0].astype(f32)
    scaled = [w * scale for w in weights[0]]

    def lead_row_col(i):
        row, col = iota((RB, GR), 0) + i * RB, iota((RB, GR), 1)
        out, part = row & (A - 1), row // A
        return (
            (out & (GR - 1)) // RA * AL + out // GR * RA + (out & (RA - 1)),
            col // RA * AL + part * RA + (col & (RA - 1)),
        )

    def build_lead(i, carry):
        row, col = lead_row_col(i)
        high, low = split(forward_entry(row, col, A, shift[0], scaled))
        lhi[pl.ds(i * RB, RB), :] = high
        llo[pl.ds(i * RB, RB), :] = low
        return carry

    lax.fori_loop(0, AH * A // RB, build_lead, 0)

    low64 = iota((1, LANES), 1) < 64

    def lead_apply(value, high, low):
        vh, vl = split(value)
        both = dot(high[...], jnp.concatenate([vh, vl], axis=1))
        out = both[:, :LANES] + both[:, LANES:]
        if low is not None:
            out = out + dot(low[...], vh)
        if AH == 1:
            return out.reshape(S, RA, LANES)
        out = jnp.where(low64, out[:A], out[A:])
        out = out + pltpu.roll(out, 64, 1)
        return jnp.where(low64, out[:GR], out[GR:]).reshape(S, RA, LANES)

    idall[pl.ds(s, 1)] = idown[...][None]
    all_bytes(idall.at[peers], id_recv.at[0])

    to_owner(lambda to: idall.at[to], idmine.at[own], id_send.at[1], id_recv.at[1])
    idmine[pl.ds(own, 1)] = idall[pl.ds(own, 1)]

    def build_hot(q):
        for j in range(4):
            at = j // BQ * BN + q * BQ + j % BQ
            ids_here = idrow[at : at + 1, :] & (QI - 1)
            hot[q, :, j * GR : (j + 1) * GR] = jnp.where(
                iota((QI, GR), 0) == ids_here, 1.0, 0.0
            ).astype(bf16)
            column = idcol[:, at : at + 1]
            quarter[q, j] = jnp.broadcast_to(column // QI, (GR, LANES))
            hot_t[q, j * GR : (j + 1) * GR, :] = jnp.where(
                iota((GR, QI), 1) == (column & (QI - 1)), 1.0, 0.0
            ).astype(bf16)

    lane_group = iota((1, LANES), 1) // GROUP

    def lead_step(q):
        all_bytes(rbuf.at[q, peers], recv_sem.at[0, q])
        fbuf[q] = lead_apply(rbuf[q].reshape(GR, LANES), lhi, llo)
        send_to_owners(lambda to: fbuf.at[q, to], gbuf.at[q, own], 1, q)
        gbuf[q, pl.ds(own, 1)] = fbuf[q, pl.ds(own, 1)]

    def add_step(q):
        all_bytes(gbuf.at[q, peers], recv_sem.at[1, q])
        value = gbuf[q].reshape(GR, LANES)
        turned = [value] + [pltpu.roll(value, GROUP * k, 1) for k in (1, 2, 3)]
        for j in range(4):
            spread = turned[(3 - j) % 4]
            for k in range(3):
                spread = jnp.where(lane_group == k, turned[(k - j) % 4], spread)
            high, low = split(jnp.where(lane_group == quarter[q, j], spread, 0.0))
            rhs[j * GR : (j + 1) * GR, 0:LANES] = high
            rhs[j * GR : (j + 1) * GR, LANES:] = low
        if q == 0:
            acc[...] = dot(hot[q], rhs[...])
        else:
            acc[...] += dot(hot[q], rhs[...])

    ahead = NQ // 2
    for q in range(ahead):
        lead_step(q)
    all_bytes(idmine.at[peers], id_recv.at[1])
    unpacked = [None] * AH
    for part in range(AH):
        packed_ids = idmine[...] if AH == 1 else idmine[:, part : part + 1]
        packed_ids = packed_ids.reshape(GR // PACK, LANES)
        wide = jnp.broadcast_to(packed_ids[:, None, :], (GR // PACK, PACK, LANES))
        mine = (iota((GR, LANES), 1) // BN) == (iota((GR, LANES), 0) & (PACK - 1))
        wide = jnp.where(mine, wide.reshape(GR, LANES), 0.0)
        for step in (BN, 2 * BN, 4 * BN):
            wide = wide + pltpu.roll(wide, step, 1)
        unpacked[part] = wide
    ids_in = unpacked[0]
    if AH == 2:
        ids_in = jnp.where((iota((1, LANES), 1) // BN) == 0, unpacked[0], unpacked[1])
    idcol[...] = ids_in.astype(jnp.int32)
    idrow[...] = jnp.transpose(ids_in).astype(jnp.int32)
    for q in range(ahead, NQ):
        build_hot(q - ahead)
        lead_step(q)
    for q in range(NQ):
        if q + NQ - ahead < NQ:
            build_hot(q + NQ - ahead)
        add_step(q)

    packed = acc[:, :LANES] + acc[:, LANES:]
    ZR = QI // ZN
    table[...] = packed.reshape(ZN, ZR, LANES)

    def send_z(k, carry):
        to = lax.rem(zz + k, ZN)
        pltpu.make_async_remote_copy(
            table.at[to],
            zrecv.at[zz],
            z_send.at[0],
            z_recv.at[0],
            device_id=(z_grid(to), s),
            device_id_type=MESH,
        ).start()
        return carry

    lax.fori_loop(1, ZN, send_z, 0)
    zrecv[pl.ds(zz, 1)] = table[pl.ds(zz, 1)]
    zpeers = pl.ds(0, ZN - 1)
    all_bytes(zrecv.at[zpeers], z_recv.at[0])
    total = zrecv[0]
    for k in range(1, ZN):
        total = total + zrecv[k]
    zsum[...] = total

    def send_sum(k, carry):
        to = lax.rem(zz + k, ZN)
        pltpu.make_async_remote_copy(
            zsum,
            tsum.at[zz],
            z_send.at[1],
            z_recv.at[1],
            device_id=(z_grid(to), s),
            device_id_type=MESH,
        ).start()
        return carry

    lax.fori_loop(1, ZN, send_sum, 0)
    tsum[pl.ds(zz, 1)] = total[None]
    def build_lead_back(i, carry):
        row, col = lead_row_col(i)
        dlead[pl.ds(i * RB, RB), :] = backward_entry(row, col).astype(bf16)
        return carry

    lax.fori_loop(0, AH * A // RB, build_lead_back, 0)

    BC = 4
    for c in range(BN // BC):
        row, col = iota((ROWS, BC * AL), 0), iota((ROWS, BC * AL), 1)
        entry = backward_entry(row & (BN - 1), col // AL + c * BC)
        entry = jnp.where(row // BN == (col & (AL - 1)), entry, 0.0)
        dsecond[c] = entry.astype(bf16)
    first = backward_entry(prow // n3, pcol // n3)
    if n3 > 1:
        first = first * backward_entry(prow & (n3 - 1), pcol & (n3 - 1))
    pxs[...] = first
    last_back = backward_entry(qrow // n5, qcol // n5) * backward_entry(
        qrow & (n5 - 1), qcol & (n5 - 1)
    )

    def build_tail_back(i, carry):
        dtail[pl.ds(i * QN, QN), :] = (pxs[pl.ds(i, 1), :] * last_back).astype(bf16)
        return carry

    lax.fori_loop(0, PN, build_tail_back, 0)
    all_bytes(tsum.at[zpeers], z_recv.at[1])
    packed = tsum[...].reshape(QI, LANES)
    high, low = split(packed)
    tsplit[:, 0:LANES] = high
    tsplit[:, LANES:] = low
    even32 = (iota((1, LANES), 1) & 32) == 0

    for q in range(NQ):
        rows_q = dot(hot_t[q], tsplit[...])
        found = []
        for j in range(4):
            row = rows_q[j * GR : (j + 1) * GR]
            row = jnp.where(lane_group == quarter[q, j], row[:, :LANES] + row[:, LANES:], 0.0)
            found.append(row + pltpu.roll(row, 64, 1))
        first = jnp.where(low64, found[0], found[2])
        last = jnp.where(low64, found[1], found[3])
        answer = jnp.where(
            even32, first + pltpu.roll(first, 96, 1), last + pltpu.roll(last, 32, 1)
        )
        abuf[q] = answer.reshape(S, RA, LANES)
        send_to_owners(lambda to: abuf.at[q, to], bbuf.at[q, own], 2, q)
        bbuf[q, pl.ds(own, 1)] = abuf[q, pl.ds(own, 1)]

    for q in range(NQ):
        all_bytes(bbuf.at[q, peers], recv_sem.at[2, q])
        obuf[q] = lead_apply(bbuf[q].reshape(GR, LANES), dlead, None)
        send_to_shards(lambda to: obuf.at[q, to], ubuf.at[q, s], 3, q)
        ubuf[q, pl.ds(s, 1)] = obuf[q, pl.ds(s, 1)]

    CR = ROWS // (BN // 4)
    for q in range(NQ):
        all_bytes(ubuf.at[q, peers], recv_sem.at[3, q])
        for p in range(PG):
            for j, tile in enumerate(swap_groups([ubuf[q, 4 * p + i] for i in range(4)])):
                vbuf[pl.ds(group_row(q, j), RA), pl.ds(p * LANES, LANES)] = tile

        if (q + 1) % AH == 0:
            at = q // AH * CR
            vh, vl = split(vbuf[at : at + CR, :])
            both = dot_t(jnp.concatenate([vh, vl], axis=0), dtail[...])
            yh, yl = split(both[:CR] + both[CR:])
            back = dsecond[q // AH]
            part = dot(back, yh) + dot(back, yl)
            if at == 0:
                out_ref[...] = part
            else:
                out_ref[...] += part
    all_bytes(idall.at[peers], id_send.at[0])
    all_bytes(idall.at[peers], id_send.at[1])
    all_bytes(table.at[zpeers], z_send.at[0])
    all_bytes(tsum.at[zpeers], z_send.at[1])
    for phase in range(4):
        for q in range(NQ):
            all_bytes(wbuf.at[q, peers], send_sem.at[phase, q])


class Config:
    pass


def run_step(cfg, x, coef, shifts, fracs, ids):
    S, ZN, AL, BN, NQ = cfg.shards, cfg.zs, cfg.rows, cfg.second, cfg.chunks
    A, TAIL, NG = cfg.lead, cfg.tail, cfg.ids
    AH, ROWS, QI = PARTS, AL * BN, NG // 4
    RA = AL // AH
    GR = S * RA
    n2, n3, n4, n5 = cfg.tail_dims
    vmem = pl.BlockSpec(memory_space=pltpu.VMEM)
    hbm = pl.BlockSpec(memory_space=pl.ANY)
    V, D = pltpu.VMEM, pltpu.SemaphoreType.DMA
    slabs = V((NQ, S, RA, LANES), f32)
    return pl.pallas_call(
        functools.partial(step_kernel, cfg),
        out_shape=jax.ShapeDtypeStruct((ROWS, TAIL), f32),
        in_specs=[hbm] * 5,
        out_specs=vmem,
        scratch_shapes=[
            pltpu.SMEM(coef.shape, coef.dtype),
            pltpu.SMEM(shifts.shape, shifts.dtype),
            pltpu.SMEM(fracs.shape, fracs.dtype),
            V(ids.shape, ids.dtype),
            V((ROWS, TAIL), f32),
            V((AH * A, GR), bf16),
            V((BN // 4, ROWS, 4 * AL), bf16),
            V((TAIL, TAIL), bf16),
            V((ROWS, ROWS), bf16),
            V((ROWS, ROWS), bf16),
            V((n2 * n3, TAIL), f32),
            V((TAIL, TAIL), bf16),
            V((TAIL, TAIL), bf16),
            V((AH * A, GR), bf16),
            V((AH * A, GR), bf16),
            V((ROWS, TAIL), f32),
            slabs,
            slabs,
            slabs,
            slabs,
            V((AL, LANES), f32),
            V((AL // PACK, LANES), f32),
            V((S, AL // PACK, LANES), f32),
            V((S, AL // PACK, LANES), f32),
            V((GR, LANES), jnp.int32),
            V((LANES, GR), jnp.int32),
            V((NQ, 4, GR, LANES), jnp.int32),
            V((NQ, QI, 4 * GR), bf16),
            V((NQ, 4 * GR, QI), bf16),
            V((4 * GR, 2 * LANES), bf16),
            V((QI, 2 * LANES), f32),
            V((ZN, QI // ZN, LANES), f32),
            V((ZN, QI // ZN, LANES), f32),
            V((QI // ZN, LANES), f32),
            V((ZN, QI // ZN, LANES), f32),
            V((QI, 2 * LANES), bf16),
            slabs,
            slabs,
            slabs,
            slabs,
            D((5,)),
            D((2,)),
            D((2,)),
            D((4, NQ)),
            D((4, NQ)),
            D((2,)),
            D((2,)),
        ],
        compiler_params=pltpu.CompilerParams(
            collective_id=0, has_side_effects=True, vmem_limit_bytes=56 * 1024 * 1024
        ),
    )(coef, shifts, fracs, x, ids)


def build(mesh, tail_dims, id_count):
    def body(density, coefficients, offsets, fractions, subspace_ids):
        _, rows, second, tail = density.shape
        cfg = Config()
        cfg.shards = mesh.shape["shard"]
        cfg.zs = mesh.shape["grid"] // cfg.shards
        cfg.rows, cfg.second, cfg.tail = rows, second, tail
        cfg.lead = rows * cfg.shards
        cfg.chunks = second * GROUP // LANES * PARTS
        cfg.tail_dims, cfg.ids = tail_dims, id_count
        out = run_step(
            cfg,
            density.reshape(rows * second, tail),
            coefficients,
            offsets,
            fractions,
            subspace_ids[0],
        )
        return out.reshape(density.shape)

    return jax.shard_map(
        body,
        mesh=mesh,
        in_specs=(
            P("grid", "shard", None, None),
            P("grid"),
            P("grid", None),
            P("grid", None),
            P("grid", "shard", None),
        ),
        out_specs=P("grid", "shard", None, None),
        check_vma=False,
    )


def solution(mesh):
    return build(mesh, TAIL_DIMS, IDS)
```

time: 98.1 us -> 83.6 us (0.85)
  Pallas kernels: 95.3 us -> 80.9 us
    pallas_call x1, Pallas kernels: 95.3 us -> 80.9 us  [run_step(): pl.pallas_call(functools.partial(step_kernel, cfg), out_shape=jax.ShapeDt...]
where the time goes in v2:
time: 83.6 us; the launch traced here: 83.4 us
  Pallas kernels  80.9 us (97%)
  local copies, waits for them, and re-layouts  1.88 us (2%)
    pallas_call x1, Pallas kernels, run_step(): pl.pallas_call(functools.partial(step_kernel, cfg), out_shape=jax.ShapeDt...  80.9 us
    unnamed x1, local copies, waits for them, and re-layouts  1.88 us

profile of v2, /device:TPU:1, one launch (start us, length us, event | category | flops | bytes accessed | tf_op | source)
XLA Modules:
  0.0 83.4 jit_solution(18394105613261045593)
XLA Ops:
  0.7 80.9 %shard_map.55 = f32[256,512]{1,0:T(8,128)} custom-call(s32[1]{0:T(128)S(6)} %copy.7.coef_hbm, s32[1,6]{1,0:T(1,128)} %shifts_hbm.1, f32[1,6]{1,0:T(1,128)} %fracs_hbm.1, f32[256,512]{1,0:T(8,128)} %bitcast.4, s32[16,16]{1,0:T(8,128)} %bitcast.5), custom_call_target="tpu_custom_call" | custom-call | tf_op jit(solution)/shard_map/pallas_call | solution.py:557
  81.5 1.9 %copy.8 = f32[1,16,16,512]{3,2,1,0:T(8,128)} copy(f32[1,16,16,512]{3,2,1,0:T(8,128)} %bitcast.3) | data formatting | bytes 1048576

commit v3 on v2

--- a/solution.py
+++ b/solution.py
@@ -9,12 +9,14 @@
 
 MESH = pl.DeviceIdType.MESH
 CORES = 2
-GROUP = 32
+HALVES = 2
+GROUP = 16
 LANES = 128
+GN = LANES // GROUP
 TAIL_DIMS = (8, 4, 4, 4)
 IDS = 1024
 PACK = 8
-PARTS = 1
+
 
 f32 = jnp.float32
 bf16 = jnp.bfloat16
@@ -74,19 +76,37 @@
 
 def swap_groups(tiles):
     lane = iota(tiles[0].shape, 1)
-    low64 = lane < 64
-    even32 = (lane & 32) == 0
-    half = [None] * 4
-    for a in (0, 1):
-        b = a + 2
-        half[a] = jnp.where(low64, tiles[a], pltpu.roll(tiles[b], 64, 1))
-        half[b] = jnp.where(low64, pltpu.roll(tiles[a], 64, 1), tiles[b])
-    done = [None] * 4
-    for a in (0, 2):
-        b = a + 1
-        done[a] = jnp.where(even32, half[a], pltpu.roll(half[b], 32, 1))
-        done[b] = jnp.where(even32, pltpu.roll(half[a], 96, 1), half[b])
-    return done
+    dist = GN // 2
+    while dist:
+        width = dist * GROUP
+        low = (lane & width) == 0
+        done = list(tiles)
+        for a in range(GN):
+            if a & dist == 0:
+                b = a + dist
+                done[a] = jnp.where(low, tiles[a], pltpu.roll(tiles[b], width, 1))
+                done[b] = jnp.where(low, pltpu.roll(tiles[a], LANES - width, 1), tiles[b])
+        tiles = done
+        dist //= 2
+    return tiles
+
+
+def sum_groups(tiles):
+    lane = iota(tiles[0].shape, 1)
+    dist = GN // 2
+    while dist:
+        width = dist * GROUP
+        low = (lane & width) == 0
+        tiles = [
+            jnp.where(
+                low,
+                tiles[a] + pltpu.roll(tiles[a], LANES - width, 1),
+                tiles[a + dist] + pltpu.roll(tiles[a + dist], width, 1),
+            )
+            for a in range(dist)
+        ]
+        dist //= 2
+    return tiles[0]
 
 
 def step_kernel(
@@ -148,9 +168,9 @@
     S, ZN, AL, BN, NQ = cfg.shards, cfg.zs, cfg.rows, cfg.second, cfg.chunks
     A, TAIL = cfg.lead, cfg.tail
     ROWS = AL * BN
-    AH, NG = PARTS, cfg.ids
-    RA, BQ, QI = AL // AH, 4 // AH, NG // 4
-    GR = S * RA
+    NG = cfg.ids
+    BH, QI = BN // GN, NG // GN
+    GR = S * AL
     g = lax.axis_index("grid")
     s = lax.axis_index("shard")
     core = lax.rem(g, CORES)
@@ -250,8 +270,9 @@
 
     def build_tail(i, carry):
         high, low = split(pxs[pl.ds(i, 1), :] * last)
-        thi[pl.ds(i * QN, QN), :] = high
-        tlo[pl.ds(i * QN, QN), :] = low
+        at = (lax.rem(i, HALVES) * (PN // HALVES) + i // HALVES) * QN
+        thi[pl.ds(at, QN), :] = high
+        tlo[pl.ds(at, QN), :] = low
         return carry
 
     lax.fori_loop(0, PN, build_tail, 0)
@@ -299,18 +320,19 @@
 
     peers = pl.ds(0, S - 1)
 
-    PG = TAIL // LANES
+    HALF = TAIL // HALVES
 
     def group_row(q, j):
-        return (q * BQ + j % BQ) * AL + j // BQ * RA
+        return (q % BH * GN + j) * AL
+
+    def group_lanes(q, p):
+        return pl.ds(q // BH * HALF + p * LANES, LANES)
 
     for q in range(NQ):
-        for p in range(PG):
-            tiles = [
-                vbuf[pl.ds(group_row(q, j), RA), pl.ds(p * LANES, LANES)] for j in range(4)
-            ]
+        for p in range(HALF // LANES):
+            tiles = [vbuf[pl.ds(group_row(q, j), AL), group_lanes(q, p)] for j in range(GN)]
             for i, tile in enumerate(swap_groups(tiles)):
-                wbuf[q, 4 * p + i] = tile
+                wbuf[q, GN * p + i] = tile
         send_to_shards(lambda to: wbuf.at[q, to], rbuf.at[q, s], 0, q)
         rbuf[q, pl.ds(s, 1)] = wbuf[q, pl.ds(s, 1)]
 
@@ -318,12 +340,7 @@
     scaled = [w * scale for w in weights[0]]
 
     def lead_row_col(i):
-        row, col = iota((RB, GR), 0) + i * RB, iota((RB, GR), 1)
-        out, part = row & (A - 1), row // A
-        return (
-            (out & (GR - 1)) // RA * AL + out // GR * RA + (out & (RA - 1)),
-            col // RA * AL + part * RA + (col & (RA - 1)),
-        )
+        return iota((RB, A), 0) + i * RB, iota((RB, A), 1)
 
     def build_lead(i, carry):
         row, col = lead_row_col(i)
@@ -332,9 +349,7 @@
         llo[pl.ds(i * RB, RB), :] = low
         return carry
 
-    lax.fori_loop(0, AH * A // RB, build_lead, 0)
-
-    low64 = iota((1, LANES), 1) < 64
+    lax.fori_loop(0, A // RB, build_lead, 0)
 
     def lead_apply(value, high, low):
         vh, vl = split(value)
@@ -342,11 +357,7 @@
         out = both[:, :LANES] + both[:, LANES:]
         if low is not None:
             out = out + dot(low[...], vh)
-        if AH == 1:
-            return out.reshape(S, RA, LANES)
-        out = jnp.where(low64, out[:A], out[A:])
-        out = out + pltpu.roll(out, 64, 1)
-        return jnp.where(low64, out[:GR], out[GR:]).reshape(S, RA, LANES)
+        return out.reshape(S, AL, LANES)
 
     idall[pl.ds(s, 1)] = idown[...][None]
     all_bytes(idall.at[peers], id_recv.at[0])
@@ -354,16 +365,16 @@
     to_owner(lambda to: idall.at[to], idmine.at[own], id_send.at[1], id_recv.at[1])
     idmine[pl.ds(own, 1)] = idall[pl.ds(own, 1)]
 
-    def build_hot(q):
-        for j in range(4):
-            at = j // BQ * BN + q * BQ + j % BQ
+    def build_hot(h):
+        for j in range(GN):
+            at = h * GN + j
             ids_here = idrow[at : at + 1, :] & (QI - 1)
-            hot[q, :, j * GR : (j + 1) * GR] = jnp.where(
+            hot[h, :, j * GR : (j + 1) * GR] = jnp.where(
                 iota((QI, GR), 0) == ids_here, 1.0, 0.0
             ).astype(bf16)
             column = idcol[:, at : at + 1]
-            quarter[q, j] = jnp.broadcast_to(column // QI, (GR, LANES))
-            hot_t[q, j * GR : (j + 1) * GR, :] = jnp.where(
+            quarter[h, j] = jnp.broadcast_to(column // QI, (GR, LANES))
+            hot_t[h, j * GR : (j + 1) * GR, :] = jnp.where(
                 iota((GR, QI), 1) == (column & (QI - 1)), 1.0, 0.0
             ).astype(bf16)
 
@@ -377,102 +388,121 @@
 
     def add_step(q):
         all_bytes(gbuf.at[q, peers], recv_sem.at[1, q])
+        half, h = q // BH, q % BH
         value = gbuf[q].reshape(GR, LANES)
-        turned = [value] + [pltpu.roll(value, GROUP * k, 1) for k in (1, 2, 3)]
-        for j in range(4):
-            spread = turned[(3 - j) % 4]
-            for k in range(3):
-                spread = jnp.where(lane_group == k, turned[(k - j) % 4], spread)
-            high, low = split(jnp.where(lane_group == quarter[q, j], spread, 0.0))
-            rhs[j * GR : (j + 1) * GR, 0:LANES] = high
-            rhs[j * GR : (j + 1) * GR, LANES:] = low
-        if q == 0:
-            acc[...] = dot(hot[q], rhs[...])
+        for at in range(0, GR, RB):
+            here = value[at : at + RB]
+            turned = [here] + [pltpu.roll(here, GROUP * k, 1) for k in range(1, GN)]
+            for j in range(GN):
+                spread = turned[(GN - 1 - j) % GN]
+                for k in range(GN - 1):
+                    spread = jnp.where(lane_group == k, turned[(k - j) % GN], spread)
+                mine = lane_group == quarter[h, j, at : at + RB]
+                high, low = split(jnp.where(mine, spread, 0.0))
+                rhs[j * GR + at : j * GR + at + RB, 0:LANES] = high
+                rhs[j * GR + at : j * GR + at + RB, LANES:] = low
+        if h == 0:
+            acc[half] = dot(hot[h], rhs[...])
         else:
-            acc[...] += dot(hot[q], rhs[...])
+            acc[half] += dot(hot[h], rhs[...])
 
     ahead = NQ // 2
     for q in range(ahead):
         lead_step(q)
     all_bytes(idmine.at[peers], id_recv.at[1])
-    unpacked = [None] * AH
-    for part in range(AH):
-        packed_ids = idmine[...] if AH == 1 else idmine[:, part : part + 1]
-        packed_ids = packed_ids.reshape(GR // PACK, LANES)
-        wide = jnp.broadcast_to(packed_ids[:, None, :], (GR // PACK, PACK, LANES))
-        mine = (iota((GR, LANES), 1) // BN) == (iota((GR, LANES), 0) & (PACK - 1))
-        wide = jnp.where(mine, wide.reshape(GR, LANES), 0.0)
-        for step in (BN, 2 * BN, 4 * BN):
-            wide = wide + pltpu.roll(wide, step, 1)
-        unpacked[part] = wide
-    ids_in = unpacked[0]
-    if AH == 2:
-        ids_in = jnp.where((iota((1, LANES), 1) // BN) == 0, unpacked[0], unpacked[1])
+    packed_ids = idmine[...].reshape(GR // PACK, LANES)
+    ids_in = jnp.broadcast_to(packed_ids[:, None, :], (GR // PACK, PACK, LANES))
+    mine = (iota((GR, LANES), 1) // BN) == (iota((GR, LANES), 0) & (PACK - 1))
+    ids_in = jnp.where(mine, ids_in.reshape(GR, LANES), 0.0)
+    for step in (BN, 2 * BN, 4 * BN):
+        ids_in = ids_in + pltpu.roll(ids_in, step, 1)
     idcol[...] = ids_in.astype(jnp.int32)
     idrow[...] = jnp.transpose(ids_in).astype(jnp.int32)
     for q in range(ahead, NQ):
         build_hot(q - ahead)
         lead_step(q)
-    for q in range(NQ):
-        if q + NQ - ahead < NQ:
-            build_hot(q + NQ - ahead)
-        add_step(q)
-
-    packed = acc[:, :LANES] + acc[:, LANES:]
+
     ZR = QI // ZN
-    table[...] = packed.reshape(ZN, ZR, LANES)
-
-    def send_z(k, carry):
-        to = lax.rem(zz + k, ZN)
-        pltpu.make_async_remote_copy(
-            table.at[to],
-            zrecv.at[zz],
-            z_send.at[0],
-            z_recv.at[0],
-            device_id=(z_grid(to), s),
-            device_id_type=MESH,
-        ).start()
-        return carry
-
-    lax.fori_loop(1, ZN, send_z, 0)
-    zrecv[pl.ds(zz, 1)] = table[pl.ds(zz, 1)]
     zpeers = pl.ds(0, ZN - 1)
-    all_bytes(zrecv.at[zpeers], z_recv.at[0])
-    total = zrecv[0]
-    for k in range(1, ZN):
-        total = total + zrecv[k]
-    zsum[...] = total
-
-    def send_sum(k, carry):
-        to = lax.rem(zz + k, ZN)
-        pltpu.make_async_remote_copy(
-            zsum,
-            tsum.at[zz],
-            z_send.at[1],
-            z_recv.at[1],
-            device_id=(z_grid(to), s),
-            device_id_type=MESH,
-        ).start()
-        return carry
-
-    lax.fori_loop(1, ZN, send_sum, 0)
-    tsum[pl.ds(zz, 1)] = total[None]
+
+    def to_z(src, dst, at):
+        def send(k, carry):
+            to = lax.rem(zz + ZN - k, ZN)
+            pltpu.make_async_remote_copy(
+                src(to),
+                dst,
+                z_send.at[at],
+                z_recv.at[at],
+                device_id=(z_grid(to), s),
+                device_id_type=MESH,
+            ).start()
+            return carry
+
+        lax.fori_loop(1, ZN, send, 0)
+
+    def sum_start(half):
+        packed = acc[half, :, :LANES] + acc[half, :, LANES:]
+        table[half] = packed.reshape(ZN, ZR, LANES)
+        to_z(lambda to: table.at[half, to], zrecv.at[half, zz], 2 * half)
+        zrecv[half, pl.ds(zz, 1)] = table[half, pl.ds(zz, 1)]
+
+    def sum_middle(half):
+        all_bytes(zrecv.at[half, zpeers], z_recv.at[2 * half])
+        total = zrecv[half, 0]
+        for k in range(1, ZN):
+            total = total + zrecv[half, k]
+        zsum[half] = total
+        to_z(lambda to: zsum.at[half], tsum.at[half, zz], 2 * half + 1)
+        tsum[half, pl.ds(zz, 1)] = total[None]
+
+    def sum_end(half):
+        all_bytes(tsum.at[half, zpeers], z_recv.at[2 * half + 1])
+        high, low = split(tsum[half].reshape(QI, LANES))
+        tsplit[half, :, 0:LANES] = high
+        tsplit[half, :, LANES:] = low
+
+    def answer_step(q):
+        half, h = q // BH, q % BH
+        rows_q = dot(hot_t[h], tsplit[half])
+        found = []
+        for j in range(GN):
+            row = rows_q[j * GR : (j + 1) * GR]
+            found.append(
+                jnp.where(lane_group == quarter[h, j], row[:, :LANES] + row[:, LANES:], 0.0)
+            )
+        abuf[q] = sum_groups(found).reshape(S, AL, LANES)
+        send_to_owners(lambda to: abuf.at[q, to], bbuf.at[q, own], 2, q)
+        bbuf[q, pl.ds(own, 1)] = abuf[q, pl.ds(own, 1)]
+
+    add_step(0)
+    add_step(1)
+    sum_start(0)
+    add_step(2)
+    sum_middle(0)
+    add_step(3)
+    sum_start(1)
+    sum_end(0)
+    answer_step(0)
+    sum_middle(1)
+    answer_step(1)
     def build_lead_back(i, carry):
         row, col = lead_row_col(i)
         dlead[pl.ds(i * RB, RB), :] = backward_entry(row, col).astype(bf16)
         return carry
 
-    lax.fori_loop(0, AH * A // RB, build_lead_back, 0)
-
-    BC = 4
+    lax.fori_loop(0, A // RB, build_lead_back, 0)
+
+    BC = GN
     for c in range(BN // BC):
         row, col = iota((ROWS, BC * AL), 0), iota((ROWS, BC * AL), 1)
         entry = backward_entry(row & (BN - 1), col // AL + c * BC)
         entry = jnp.where(row // BN == (col & (AL - 1)), entry, 0.0)
         dsecond[c] = entry.astype(bf16)
-    first = backward_entry(prow // n3, pcol // n3)
+    spot = iota((PN, TAIL), 1)
+    pback = spot % HALF // QN * HALVES + spot // HALF
+    first = backward_entry(prow // n3, pback // n3)
     if n3 > 1:
-        first = first * backward_entry(prow & (n3 - 1), pcol & (n3 - 1))
+        first = first * backward_entry(prow & (n3 - 1), pback & (n3 - 1))
     pxs[...] = first
     last_back = backward_entry(qrow // n5, qcol // n5) * backward_entry(
         qrow & (n5 - 1), qcol & (n5 - 1)
@@ -483,28 +513,9 @@
         return carry
 
     lax.fori_loop(0, PN, build_tail_back, 0)
-    all_bytes(tsum.at[zpeers], z_recv.at[1])
-    packed = tsum[...].reshape(QI, LANES)
-    high, low = split(packed)
-    tsplit[:, 0:LANES] = high
-    tsplit[:, LANES:] = low
-    even32 = (iota((1, LANES), 1) & 32) == 0
-
-    for q in range(NQ):
-        rows_q = dot(hot_t[q], tsplit[...])
-        found = []
-        for j in range(4):
-            row = rows_q[j * GR : (j + 1) * GR]
-            row = jnp.where(lane_group == quarter[q, j], row[:, :LANES] + row[:, LANES:], 0.0)
-            found.append(row + pltpu.roll(row, 64, 1))
-        first = jnp.where(low64, found[0], found[2])
-        last = jnp.where(low64, found[1], found[3])
-        answer = jnp.where(
-            even32, first + pltpu.roll(first, 96, 1), last + pltpu.roll(last, 32, 1)
-        )
-        abuf[q] = answer.reshape(S, RA, LANES)
-        send_to_owners(lambda to: abuf.at[q, to], bbuf.at[q, own], 2, q)
-        bbuf[q, pl.ds(own, 1)] = abuf[q, pl.ds(own, 1)]
+    sum_end(1)
+    answer_step(2)
+    answer_step(3)
 
     for q in range(NQ):
         all_bytes(bbuf.at[q, peers], recv_sem.at[2, q])
@@ -512,28 +523,27 @@
         send_to_shards(lambda to: obuf.at[q, to], ubuf.at[q, s], 3, q)
         ubuf[q, pl.ds(s, 1)] = obuf[q, pl.ds(s, 1)]
 
-    CR = ROWS // (BN // 4)
+    CR = GN * AL
     for q in range(NQ):
         all_bytes(ubuf.at[q, peers], recv_sem.at[3, q])
-        for p in range(PG):
-            for j, tile in enumerate(swap_groups([ubuf[q, 4 * p + i] for i in range(4)])):
-                vbuf[pl.ds(group_row(q, j), RA), pl.ds(p * LANES, LANES)] = tile
-
-        if (q + 1) % AH == 0:
-            at = q // AH * CR
-            vh, vl = split(vbuf[at : at + CR, :])
-            both = dot_t(jnp.concatenate([vh, vl], axis=0), dtail[...])
-            yh, yl = split(both[:CR] + both[CR:])
-            back = dsecond[q // AH]
-            part = dot(back, yh) + dot(back, yl)
-            if at == 0:
-                out_ref[...] = part
-            else:
-                out_ref[...] += part
+        for p in range(HALF // LANES):
+            tiles = [ubuf[q, GN * p + i] for i in range(GN)]
+            for j, tile in enumerate(swap_groups(tiles)):
+                vbuf[pl.ds(group_row(q, j), AL), group_lanes(q, p)] = tile
+        lanes = slice(q // BH * HALF, (q // BH + 1) * HALF)
+        vh, vl = split(vbuf[q % BH * CR : (q % BH + 1) * CR, lanes])
+        both = dot_t(jnp.concatenate([vh, vl], axis=0), dtail[:, lanes])
+        yh, yl = split(both[:CR] + both[CR:])
+        part = dot(dsecond[q % BH], yh) + dot(dsecond[q % BH], yl)
+        if q == 0:
+            out_ref[...] = part
+        else:
+            out_ref[...] += part
     all_bytes(idall.at[peers], id_send.at[0])
     all_bytes(idall.at[peers], id_send.at[1])
-    all_bytes(table.at[zpeers], z_send.at[0])
-    all_bytes(tsum.at[zpeers], z_send.at[1])
+    for half in range(HALVES):
+        all_bytes(table.at[half, zpeers], z_send.at[2 * half])
+        all_bytes(tsum.at[half, zpeers], z_send.at[2 * half + 1])
     for phase in range(4):
         for q in range(NQ):
             all_bytes(wbuf.at[q, peers], send_sem.at[phase, q])
@@ -546,17 +556,16 @@
 def run_step(cfg, x, coef, shifts, fracs, ids):
     S, ZN, AL, BN, NQ = cfg.shards, cfg.zs, cfg.rows, cfg.second, cfg.chunks
     A, TAIL, NG = cfg.lead, cfg.tail, cfg.ids
-    AH, ROWS, QI = PARTS, AL * BN, NG // 4
-    RA = AL // AH
-    GR = S * RA
+    ROWS, QI, BH = AL * BN, NG // GN, BN // GN
+    GR = S * AL
     n2, n3, n4, n5 = cfg.tail_dims
     vmem = pl.BlockSpec(memory_space=pltpu.VMEM)
     hbm = pl.BlockSpec(memory_space=pl.ANY)
     V, D = pltpu.VMEM, pltpu.SemaphoreType.DMA
-    slabs = V((NQ, S, RA, LANES), f32)
+    slabs = V((NQ, S, AL, LANES), f32)
     return pl.pallas_call(
         functools.partial(step_kernel, cfg),
-        out_shape=jax.ShapeDtypeStruct((ROWS, TAIL), f32),
+        out_shape=pltpu.VMEM((ROWS, TAIL), f32),
         in_specs=[hbm] * 5,
         out_specs=vmem,
         scratch_shapes=[
@@ -565,16 +574,16 @@
             pltpu.SMEM(fracs.shape, fracs.dtype),
             V(ids.shape, ids.dtype),
             V((ROWS, TAIL), f32),
-            V((AH * A, GR), bf16),
-            V((BN // 4, ROWS, 4 * AL), bf16),
+            V((A, A), bf16),
+            V((BH, ROWS, GN * AL), bf16),
             V((TAIL, TAIL), bf16),
             V((ROWS, ROWS), bf16),
             V((ROWS, ROWS), bf16),
             V((n2 * n3, TAIL), f32),
             V((TAIL, TAIL), bf16),
             V((TAIL, TAIL), bf16),
-            V((AH * A, GR), bf16),
-            V((AH * A, GR), bf16),
+            V((A, A), bf16),
+            V((A, A), bf16),
             V((ROWS, TAIL), f32),
             slabs,
             slabs,
@@ -586,16 +595,16 @@
             V((S, AL // PACK, LANES), f32),
             V((GR, LANES), jnp.int32),
             V((LANES, GR), jnp.int32),
-            V((NQ, 4, GR, LANES), jnp.int32),
-            V((NQ, QI, 4 * GR), bf16),
-            V((NQ, 4 * GR, QI), bf16),
-            V((4 * GR, 2 * LANES), bf16),
-            V((QI, 2 * LANES), f32),
-            V((ZN, QI // ZN, LANES), f32),
-            V((ZN, QI // ZN, LANES), f32),
-            V((QI // ZN, LANES), f32),
-            V((ZN, QI // ZN, LANES), f32),
-            V((QI, 2 * LANES), bf16),
+            V((BH, GN, GR, LANES), jnp.int32),
+            V((BH, QI, GN * GR), bf16),
+            V((BH, GN * GR, QI), bf16),
+            V((GN * GR, 2 * LANES), bf16),
+            V((HALVES, QI, 2 * LANES), f32),
+            V((HALVES, ZN, QI // ZN, LANES), f32),
+            V((HALVES, ZN, QI // ZN, LANES), f32),
+            V((HALVES, QI // ZN, LANES), f32),
+            V((HALVES, ZN, QI // ZN, LANES), f32),
+            V((HALVES, QI, 2 * LANES), bf16),
             slabs,
             slabs,
             slabs,
@@ -605,8 +614,8 @@
             D((2,)),
             D((4, NQ)),
             D((4, NQ)),
-            D((2,)),
-            D((2,)),
+            D((2 * HALVES,)),
+            D((2 * HALVES,)),
         ],
         compiler_params=pltpu.CompilerParams(
             collective_id=0, has_side_effects=True, vmem_limit_bytes=56 * 1024 * 1024
@@ -622,7 +631,7 @@
         cfg.zs = mesh.shape["grid"] // cfg.shards
         cfg.rows, cfg.second, cfg.tail = rows, second, tail
         cfg.lead = rows * cfg.shards
-        cfg.chunks = second * GROUP // LANES * PARTS
+        cfg.chunks = HALVES * second * GROUP // LANES
         cfg.tail_dims, cfg.ids = tail_dims, id_count
         out = run_step(
             cfg,

time: 83.6 us -> 78 us (0.933)
  Pallas kernels: 80.9 us -> 76.4 us
  local copies, waits for them, and re-layouts: 1.88 us -> 0.8 us
    pallas_call x1, Pallas kernels: 80.9 us -> 76.4 us  [run_step(): pl.pallas_call(functools.partial(step_kernel, cfg), out_shape=pltpu.VMEM(...]
    unnamed x1, local copies, waits for them, and re-layouts: 1.88 us -> 0.8 us
where the time goes in v3:
time: 78 us; the launch traced here: 77.8 us
  Pallas kernels  76.4 us (98%)
  local copies, waits for them, and re-layouts  0.8 us (1%)
    pallas_call x1, Pallas kernels, run_step(): pl.pallas_call(functools.partial(step_kernel, cfg), out_shape=pltpu.VMEM(...  76.4 us

profile of v3, /device:TPU:1, one launch (start us, length us, event | category | flops | bytes accessed | tf_op | source)
XLA Modules:
  0.0 77.8 jit_solution(12257480947477934097)
XLA Ops:
  0.7 76.4 %shard_map.55 = f32[256,512]{1,0:T(8,128)S(1)} custom-call(s32[1]{0:T(128)S(6)} %copy.8.coef_hbm, s32[1,6]{1,0:T(1,128)} %shifts_hbm.1, f32[1,6]{1,0:T(1,128)} %fracs_hbm.1, f32[256,512]{1,0:T(8,128)} %bitcast.4, s32[16,16]{1,0:T(8,128)} %bitcast.5), custom_call_target="tpu_custom_call" | custom-call | tf_op jit(solution)/shard_map/pallas_call | solution.py:566
  77.0 0.8 %copy.7 = f32[1,16,16,512]{3,2,1,0:T(8,128)} copy(f32[1,16,16,512]{3,2,1,0:T(8,128)S(1)} %bitcast.3) | data formatting | bytes 1048576
